TPU v7x, 32 devices: a whole 2x2x4 slice. The times are simulated.
32 devices in a mesh: rows: 32 (over z, y, x, core).
Axes of the slice: x: 2, y: 2, z: 4, core: 2. Of those that a mesh axis runs over, the one named last changes fastest.
Arguments:
- snapshots: float32 [16384, 512], P('rows'), may hold values from -100 to 100
- validation: float32 [16384, 512], P('rows'), may hold values from -100 to 100
- eigenvectors: float32 [512, 64], replicated, may hold values from -0.25 to 0.25
- eigenvalues: float32 [64], replicated, may hold values from 16 to 256
Outputs:
- gram: float32 [512, 512], replicated
- modes: float32 [64, 16384], P(None, 'rows')
- train_coef: float32 [64, 512], replicated
- valid_coef: float32 [64, 512], replicated
All inputs are finite; a program needn't handle non-finite values.
Results may differ from a plain program's by a relative error of at most 0.000071.
Values sent between devices are 32-bit elements; how exact they have to be, the bound alone decides.
No kernel may reach another device: no remote copies, remote signals or barrier semaphores. Data moves between devices by JAX's collectives and lax.ppermute only.
A program may use at most 64 MiB of HBM per device.

v0:
```python
import jax
import jax.numpy as jnp
from jax import lax
from jax.sharding import PartitionSpec as P


def body(snapshots, validation, eigenvectors, eigenvalues):
    highest = lax.Precision.HIGHEST
    devices = lax.axis_size("rows")
    total = snapshots.shape[0] * devices * 1.0
    gram_part = (
        lax.dot_general(
            snapshots,
            snapshots,
            (((0,), (0,)), ((), ())),
            precision=highest,
            preferred_element_type=jnp.float32,
        )
        / total
    )
    scales = lax.rsqrt(eigenvalues)
    modes = (
        lax.dot_general(
            eigenvectors,
            snapshots,
            (((0,), (1,)), ((), ())),
            precision=highest,
            preferred_element_type=jnp.float32,
        )
        * scales[:, None]
    )
    gram = lax.psum(gram_part, "rows")
    valid_part = (
        jnp.dot(modes, validation, precision=highest, preferred_element_type=jnp.float32) / total
    )
    valid_coef = lax.psum(valid_part, "rows")
    train_coef = (
        lax.dot_general(
            eigenvectors,
            gram,
            (((0,), (0,)), ((), ())),
            precision=highest,
            preferred_element_type=jnp.float32,
        )
        * scales[:, None]
    )
    return (gram, modes, train_coef, valid_coef)


def solution(mesh):
    in_specs = (P("rows", None), P("rows", None), P(), P())
    out_specs = (P(), P(None, "rows"), P(), P())
    return jax.shard_map(body, mesh=mesh, in_specs=in_specs, out_specs=out_specs, check_vma=False)
```

profile of v0, /device:TPU:0, one launch (start us, length us, event | category | flops | bytes accessed | tf_op | source)
XLA Modules:
  0.0 159.9 jit_solution(1666710015621987377)
XLA Ops:
  7.2 0.0 copy-start
  7.2 0.0 all-reduce.3.cloned.1.call-start
  7.2 0.7 rsqrt.3
  8.0 0.4 copy-done
  8.4 0.0 copy-start.3
  8.4 2.8 %convolution_multiply_fusion = f32[512,512]{1,0:T(8,128)} fusion(f32[512,512]{1,0:T(8,128)S(1)} %copy-done), kind=kOutput, calls=%fused_computation | convolution fusion | flops 1610874880 | bytes 2097152 | tf_op jit(solution)/shard_map/dot_general | solution.py:12
  11.2 0.0 copy-done.3
  11.2 0.0 copy-start.2
  11.2 1.1 convolution_multiply_fusion.3
  12.4 0.1 copy-done.2
  12.5 0.0 copy-start.4
  12.5 1.4 convolution_multiply_fusion.1
  13.9 0.0 copy-done.4
  13.9 0.0 all-reduce.3.cloned.1.call-update
  13.9 134.7 %all-reduce.3.cloned.1.call-done = (f32[512,512]{1,0:T(8,128)}, f32[64,512]{1,0:T(8,128)}) async-done(((f32[512,512]{1,0:T(8,128)}, f32[64,512]{1,0:T(8,128)}), (f32[512,512]{1,0:T(8,128)}, f32[64,512]{1,0:T(8,128)})) %all-reduce.3.cloned.1.call-update) | async-done | bytes 1179664 | tf_op jit(solution)/shard_map/psum | solution.py:32
  148.7 0.0 copy-start.1
  148.7 2.8 %fusion = f32[64,512]{1,0:T(8,128)} fusion(f32[512,512]{1,0:T(8,128)} %get-tuple-element.6, f32[512,64]{0,1:T(8,128)S(1)} %copy-done.3, f32[64]{0:T(128)S(1)} %rsqrt.3), kind=kOutput, calls=%fused_computation.3 | convolution fusion | flops 201359360 | bytes 1310976 | tf_op jit(solution)/shard_map/dot_general | solution.py:38
  151.4 0.0 copy-done.1
  151.4 0.0 copy-start.5
  151.4 1.0 copy.10
  152.4 0.1 copy-done.5
  152.4 0.7 copy.11
Async XLA Ops:
  7.2 1.2 copy-start
  7.2 141.5 %all-reduce.3.cloned.1.call-start = ((), (), s32[]{:S(2)}) async-start(), calls=%async_computation | async-start | bytes 2359296 | tf_op jit(solution)/shard_map/psum | solution.py:32
  8.4 2.8 %copy-start.3 = (f32[512,64]{0,1:T(8,128)S(1)}, f32[512,64]{0,1:T(8,128)}, u32[]{:S(2)}) copy-start(f32[512,64]{0,1:T(8,128)} %param.6) | copy-start | bytes 393220
  11.2 1.2 copy-start.2
  12.5 1.4 copy-start.4
  148.7 2.8 %copy-start.1 = (f32[512,512]{1,0:T(8,128)S(1)}, f32[512,512]{1,0:T(8,128)}, u32[]{:S(2)}) copy-start(f32[512,512]{1,0:T(8,128)} %get-tuple-element.6) | copy-start | bytes 3145732
  151.4 1.0 copy-start.5
Sparse Core Ops, SparseCore 0:
  14.0 134.5 all-reduce.2
where the time goes:
time: 160 us
  waiting for transfers between devices  135 us (84%)
  between operations  14 us (9%)
  matrix products  8.12 us (5%)
  local copies, waits for them, and re-layouts  2.99 us (2%)
    psum x1, waiting for transfers between devices, body(): gram = lax.psum(gram_part, 'rows')  135 us
  transfers between devices with their start and end apart: 1, of which 1 were waited for; matrix products, arithmetic and copies ran while one was open for 0% of the time, Pallas kernels for 0%

commit v1 on v0

--- a/solution.py
+++ b/solution.py
@@ -29,7 +29,7 @@
         )
         * scales[:, None]
     )
-    gram = lax.psum(gram_part, "rows")
+    gram = jnp.sum(lax.all_gather(gram_part, "rows"), axis=0)
     valid_part = (
         jnp.dot(modes, validation, precision=highest, preferred_element_type=jnp.float32) / total
     )

time: 160 us -> 346 us (2.16)
  waiting for transfers between devices: 135 us -> 307 us
  other arithmetic: 0 us -> 12.3 us
    all_gather x0 -> x1, waiting for transfers between devices: none -> 192 us  [body(): gram = jnp.sum(lax.all_gather(gram_part, 'rows'), axis=0)]
    psum x1, waiting for transfers between devices: 135 us -> 115 us  [body(): valid_coef = lax.psum(valid_part, 'rows')]
    reduce_sum x0 -> x1, other arithmetic: none -> 12.3 us  [body(): gram = jnp.sum(lax.all_gather(gram_part, 'rows'), axis=0)]
  transfers between devices with their start and end apart: 1 -> 2, of which waited for: 1 -> 2; matrix products, arithmetic and copies ran while one was open for 0% -> 6% of each run, Pallas kernels for 0% -> 0%
where the time goes in v1:
time: 346 us
  waiting for transfers between devices  307 us (89%)
  between operations  14.1 us (4%)
  other arithmetic  12.3 us (4%)
  matrix products  8.98 us (3%)
    all_gather x1, waiting for transfers between devices, body(): gram = jnp.sum(lax.all_gather(gram_part, 'rows'), axis=0)  192 us
    psum x1, waiting for transfers between devices, body(): valid_coef = lax.psum(valid_part, 'rows')  115 us
    reduce_sum x1, other arithmetic, body(): gram = jnp.sum(lax.all_gather(gram_part, 'rows'), axis=0)  12.3 us
  transfers between devices with their start and end apart: 2, of which 2 were waited for; matrix products, arithmetic and copies ran while one was open for 6% of the time, Pallas kernels for 0%

profile of v1, /device:TPU:0, one launch (start us, length us, event | category | flops | bytes accessed | tf_op | source)
XLA Modules:
  0.0 345.6 jit_solution(9090806711448041527)
XLA Ops:
  7.2 0.0 copy-start
  7.2 0.0 copy-start.2
  7.2 0.0 all-gather.3.cloned.1.call-start
  7.2 1.2 copy-done
  8.4 2.8 convolution_multiply_fusion
  11.2 0.0 all-gather.3.cloned.1.call-update
  11.3 0.0 all-reduce.2.cloned.1.call-start
  11.3 0.7 rsqrt.3
  12.0 2.0 convolution_multiply_fusion.3
  14.0 0.0 copy-start.3
  14.0 2.7 convolution_multiply_fusion.1
  16.7 0.0 all-reduce.2.cloned.1.call-update
  16.7 191.7 %all-gather.3.cloned.1.call-done = f32[16384,512]{1,0:T(8,128)} async-done(((f32[512,512]{1,0:T(8,128)}), f32[16384,512]{1,0:T(8,128)}) %all-gather.3.cloned.1.call-update) | async-done | bytes 33554448 | tf_op jit(solution)/shard_map/all_gather | solution.py:32
  208.4 12.3 %reduce_sum.9 = f32[512,512]{1,0:T(8,128)S(1)} reduce(f32[32,512,512]{2,1,0:T(8,128)} %bitcast.11, f32[]{:T(128)} %constant.6.clone.1), dimensions={0}, to_apply=%region_0.0 | reduce | flops 8126464 | bytes 34603012 | tf_op jit(solution)/shard_map/reduce_sum | solution.py:32
  220.7 0.0 copy-done.2
  220.7 0.0 copy-start.1
  220.7 1.5 fusion
  222.2 115.0 %all-reduce.2.cloned.1.call-done = f32[64,512]{1,0:T(8,128)} async-done(((f32[64,512]{1,0:T(8,128)}), f32[64,512]{1,0:T(8,128)}) %all-reduce.2.cloned.1.call-update) | async-done | bytes 131088 | tf_op jit(solution)/shard_map/psum | solution.py:36
  337.1 1.6 copy.9
  338.7 0.0 copy-done.3
  338.7 0.0 copy-done.1
Async XLA Ops:
  7.2 1.2 copy-start
  7.2 213.5 %copy-start.2 = (f32[512,64]{0,1:T(8,128)S(1)}, f32[512,64]{0,1:T(8,128)}, u32[]{:S(2)}) copy-start(f32[512,64]{0,1:T(8,128)} %param.6) | copy-start | bytes 393220
  7.2 201.2 %all-gather.3.cloned.1.call-start = ((), (), s32[]{:S(2)}) async-start(), calls=%async_computation.1 | async-start | bytes 34603008 | tf_op jit(solution)/shard_map/all_gather | solution.py:32
  11.3 325.9 %all-reduce.2.cloned.1.call-start = ((), (), s32[]{:S(2)}) async-start(), calls=%async_computation | async-start | bytes 262144 | tf_op jit(solution)/shard_map/psum | solution.py:36
  14.0 324.7 %copy-start.3 = (f32[64,512]{1,0:T(8,128)}, f32[64,512]{1,0:T(8,128)S(1)}, u32[]{:S(2)}) copy-start(f32[64,512]{1,0:T(8,128)S(1)} %convolution_multiply_fusion.3) | copy-start | bytes 393220
  220.7 118.0 %copy-start.1 = (f32[512,512]{1,0:T(8,128)}, f32[512,512]{1,0:T(8,128)S(1)}, u32[]{:S(2)}) copy-start(f32[512,512]{1,0:T(8,128)S(1)} %reduce_sum.9) | copy-start | bytes 3145732
Sparse Core Ops, SparseCore 0:
  11.4 196.9 all-gather.2
  214.5 122.5 all-reduce.1
